TPU v7x, 32 devices: a whole 2x2x4 slice. The times are simulated.
32 devices in a mesh: section: 4 (over y, x), cp: 4 (over z), tp: 2 (over core).
Axes of the slice: x: 2, y: 2, z: 4, core: 2. Of those that a mesh axis runs over, the one named last changes fastest.
Arguments:
- acts: bfloat16 [4, 512, 8192], P('section', 'cp', 'tp'), may hold values from -16 to 16
- keys: bfloat16 [4, 512, 1024], P('section', 'cp', 'tp'), may hold values from -4 to 4
- values: bfloat16 [4, 512, 1024], P('section', 'cp', 'tp'), may hold values from -6 to 6
- grads: bfloat16 [4, 512, 8192], P('section', 'cp', 'tp'), may hold values from -6 to 6
- docs: int32 [4, 512], P('section'), may hold values from 0 to 7, never falling along the last dimension, each value on 1 to 256 neighbouring positions
- order: int32 [4, 512], P('section'), may hold values from 0 to 511, each once within a row
Outputs:
- outputs: bfloat16 [4, 512, 8192], P('section', 'cp', 'tp')
- grad_query: bfloat16 [4, 512, 8192], P('section', 'cp', 'tp')
- grad_keys: bfloat16 [4, 512, 1024], P('section', 'cp', 'tp')
- grad_values: bfloat16 [4, 512, 1024], P('section', 'cp', 'tp')
Inputs may be any that keep to these rules, and one draw needn't show every extreme that they name: `docs`: along positions of one section the document numbers never fall; each document holds 1 to 256 tokens. `order`: each section's row holds every position once.
All inputs are finite; a program needn't handle non-finite values.
Results may differ from a plain program's by a relative error of at most 0.0061.
Values may be sent and summed in bfloat16 or wider, within the bound.
A program may use at most 64 MiB of HBM per device.

v0:
```python
import jax
import jax.numpy as jnp
from jax import lax
from jax.sharding import PartitionSpec as P

HEAD = 128


def passed_along(block, axis, distance):
    devices = range(lax.axis_size(axis))
    route = [((i - distance) % len(devices), i) for i in devices]
    return lax.ppermute(block, axis, route)


def split_heads(block, kv_count):
    tokens = block.shape[0]
    group = block.shape[1] // (kv_count * HEAD)
    return (
        block.reshape(tokens, kv_count, group, HEAD)
        .transpose(1, 2, 0, 3)
        .reshape(kv_count, group * tokens, HEAD)
    )


def join_heads(rows, tokens):
    kv_count = rows.shape[0]
    group = rows.shape[1] // tokens
    return (
        rows.reshape(kv_count, group, tokens, HEAD)
        .transpose(2, 0, 1, 3)
        .reshape(tokens, kv_count * group * HEAD)
    )


def forward_part(flat_q, key, value, allowed):
    scale = HEAD ** (-0.5)
    rows_q = allowed.shape[0]
    scores = (
        lax.dot_general(flat_q, key, (((1,), (1,)), ((), ())), preferred_element_type=jnp.float32)
        * scale
    )
    scores = scores.reshape(-1, rows_q, key.shape[0])
    scores = jnp.where(allowed[None], scores, -jnp.inf)
    peak = jnp.max(scores, axis=2, keepdims=True)
    expd = jnp.exp(scores - peak)
    probs = (expd / jnp.sum(expd, axis=2, keepdims=True)).astype(jnp.bfloat16)
    probs = probs.reshape(flat_q.shape[0], key.shape[0])
    attended = jnp.dot(probs, value, preferred_element_type=jnp.float32)
    return (probs, attended)


def backward_part(probs, attended, flat_g, key, value):
    scale = HEAD ** (-0.5)
    delta = jnp.sum(flat_g.astype(jnp.float32) * attended, axis=1, keepdims=True)
    dprob = lax.dot_general(
        flat_g, value, (((1,), (1,)), ((), ())), preferred_element_type=jnp.float32
    )
    dscore = (probs.astype(jnp.float32) * (dprob - delta)).astype(jnp.bfloat16)
    dquery = jnp.dot(dscore, key, preferred_element_type=jnp.float32) * scale
    return (dscore, dquery)


def key_terms(probs, dscore, flat_q, flat_g):
    scale = HEAD ** (-0.5)
    dkey = (
        lax.dot_general(
            dscore, flat_q, (((0,), (0,)), ((), ())), preferred_element_type=jnp.float32
        )
        * scale
    )
    dvalue = lax.dot_general(
        probs, flat_g, (((0,), (0,)), ((), ())), preferred_element_type=jnp.float32
    )
    return (dkey, dvalue)


def stack_terms(dkeys, dvalues):
    count = dkeys.shape[1]
    return jnp.concatenate(
        [
            dkeys.transpose(1, 0, 2).reshape(count, -1),
            dvalues.transpose(1, 0, 2).reshape(count, -1),
        ],
        axis=1,
    )


def on_device(acts, keys, values, grads, docs, order):
    tok = acts.shape[1]
    kv_count = keys.shape[2] // HEAD
    width = kv_count * HEAD
    query = passed_along(acts, "section", 1)[0]
    cotan = passed_along(grads, "section", -1)[0]
    key_all, value_all = (
        lax.all_gather(keys[0], "cp", axis=0, tiled=True),
        lax.all_gather(values[0], "cp", axis=0, tiled=True),
    )
    positions = order[0]
    doc_all = jnp.take(docs[0], positions)
    first = lax.axis_index("cp") * tok
    my_pos = lax.dynamic_slice_in_dim(positions, first, tok)
    my_doc = lax.dynamic_slice_in_dim(doc_all, first, tok)
    allowed = (my_doc[:, None] == doc_all[None, :]) & (positions[None, :] <= my_pos[:, None])
    q_rows = split_heads(query, kv_count)
    k_heads = key_all.reshape(-1, kv_count, HEAD).transpose(1, 0, 2)
    v_heads = value_all.reshape(-1, kv_count, HEAD).transpose(1, 0, 2)
    probs, attended = lax.map(
        lambda parts: forward_part(parts[0], parts[1], parts[2], allowed),
        (q_rows, k_heads, v_heads),
    )
    outputs = (query.astype(jnp.float32) + join_heads(attended, tok)).astype(jnp.bfloat16)
    g_rows = split_heads(cotan, kv_count)
    dscores, dqueries = lax.map(
        lambda parts: backward_part(parts[0], parts[1], parts[2], parts[3], parts[4]),
        (probs, attended, g_rows, k_heads, v_heads),
    )
    grad_query = (cotan.astype(jnp.float32) + join_heads(dqueries, tok)).astype(jnp.bfloat16)
    dkeys, dvalues = jax.vmap(key_terms)(probs, dscores, q_rows, g_rows)
    summed = lax.psum_scatter(stack_terms(dkeys, dvalues), "cp", scatter_dimension=0, tiled=True)
    grad_keys = summed[:, :width].astype(jnp.bfloat16)
    grad_values = summed[:, width:].astype(jnp.bfloat16)
    return (outputs[None], grad_query[None], grad_keys[None], grad_values[None])


def solution(mesh):
    placed = (
        P("section", "cp", "tp"),
        P("section", "cp", "tp"),
        P("section", "cp", "tp"),
        P("section", "cp", "tp"),
        P("section", None),
        P("section", None),
    )
    return jax.shard_map(
        on_device,
        mesh=mesh,
        in_specs=placed,
        out_specs=(
            P("section", "cp", "tp"),
            P("section", "cp", "tp"),
            P("section", "cp", "tp"),
            P("section", "cp", "tp"),
        ),
        check_vma=False,
    )
```

profile of v0, /device:TPU:0, one launch (start us, length us, event | category | flops | bytes accessed | tf_op | source)
XLA Modules:
  0.0 176.0 jit_solution(15219660777080566842)
XLA Ops:
  7.2 3.0 %collective-permute-start = (bf16[1,128,4096]{2,1,0:T(8,128)(2,1)}, bf16[1,128,4096]{2,1,0:T(8,128)(2,1)S(1)}, u32[]{:S(2)}, u32[]{:S(2)}) collective-permute-start(bf16[1,128,4096]{2,1,0:T(8,128)(2,1)} %param.10), channel_id=1, source_target_pairs={{24,0},{0,8},{8,16},{16,24},{25,1},{1,9},{9,17},{17,25},{26,2},{2,... | collective-permute-start | bytes 3145736 | tf_op jit(solution)/shard_map/ppermute | solution.py:12
  10.3 1.0 collective-permute-start.1
  11.3 1.0 copy.22
  12.3 15.2 %all-gather = bf16[1,512,512]{1,2,0:T(8,128)(2,1)S(1)} all-gather(bf16[1,128,512]{1,2,0:T(8,128)(2,1)S(1)} %copy.22), channel_id=2, replica_groups=mesh['section'=4,'cp'=4,'tp'=2] {'cp'}, dimensions={1}, use_global_device_ids=true | all-gather | bytes 655360 | tf_op jit(solution)/shard_map/all_gather | solution.py:95
  27.5 1.0 copy.25
  28.5 1.0 copy.23
  29.5 14.3 %all-gather.1 = bf16[1,512,512]{1,2,0:T(8,128)(2,1)S(1)} all-gather(bf16[1,128,512]{1,2,0:T(8,128)(2,1)S(1)} %copy.23), channel_id=3, replica_groups=mesh['section'=4,'cp'=4,'tp'=2] {'cp'}, dimensions={1}, use_global_device_ids=true | all-gather | bytes 655360 | tf_op jit(solution)/shard_map/all_gather | solution.py:96
  43.8 1.0 copy.26
  44.9 3.5 %gather_fusion = s32[512]{0:T(512)S(1)} fusion(s32[512]{0:T(512)S(1)} %bitcast.141, s32[1024]{0:T(1024)S(1)} %pad_clamp_fusion), kind=kCustom, calls=%fused_computation | custom fusion | bytes 6144 | tf_op jit(solution)/shard_map/jit(_take)/gather | solution.py:99
  48.8 0.7 copy-done.4
  49.5 1.2 copy.21
  51.2 1.5 broadcast.70.clone
  52.7 23.3 %while.26 = (s32[]{:T(128)}, bf16[4,1024,512]{1,2,0:T(8,128)(2,1)}, f32[4,1024,128]{2,1,0:T(8,128)}, bf16[4,1024,128]{1,2,0:T(8,128)(2,1)S(1)}, bf16[4,512,128]{...) while((s32[]{:T(128)}, bf16[4,1024,512]{1,2,0:T(8,128)(2,1)}, ...), condition=%wide.region_3.4_spmd.clone, body=%wide.region_0.3_spmd.clone.sunk | while | flops 274397184 | bytes 11701869 | solution.py:107
  53.2 1.5 fusion.43
  55.0 2.3 %fusion.45 = f32[4,1024,128]{2,1,0:T(8,128)} fusion(f32[4,1024,128]{2,1,0:T(8,128)} %get-tuple-element.324, s32[]{:T(128)} %get-tuple-element.322, bf16[4,512,128]{2,1,0:T(8,128)(2,1)} %get-tuple-element.338, f32[1024,512]{0,1:T(8,128)S(1)} %get-tuple-element.309, f32[1024]{0:T(1024)S(1)} %fusion.44, f32[1024]{0:T(1024)S(1)} %get-tuple-element.310), kind=kOutput, calls=%fused_computation.24.clone.1 | convolution fusion | flops 135790592 | bytes 2761728 | tf_op jit(solution)/shard_map/while/body/eval_jaxpr/dot_general | solution.py:48
  57.2 1.3 bitcast_dynamic-update-slice_fusion.5
  59.0 1.4 fusion.43
  60.8 2.3 %fusion.45 = f32[4,1024,128]{2,1,0:T(8,128)} fusion(f32[4,1024,128]{2,1,0:T(8,128)} %get-tuple-element.324, s32[]{:T(128)} %get-tuple-element.322, bf16[4,512,128]{2,1,0:T(8,128)(2,1)} %get-tuple-element.338, f32[1024,512]{0,1:T(8,128)S(1)} %get-tuple-element.309, f32[1024]{0:T(1024)S(1)} %fusion.44, f32[1024]{0:T(1024)S(1)} %get-tuple-element.310), kind=kOutput, calls=%fused_computation.24.clone.1 | convolution fusion | flops 135790592 | bytes 2761728 | tf_op jit(solution)/shard_map/while/body/eval_jaxpr/dot_general | solution.py:48
  63.0 1.3 bitcast_dynamic-update-slice_fusion.5
  64.8 1.5 fusion.43
  66.6 2.2 %fusion.45 = f32[4,1024,128]{2,1,0:T(8,128)} fusion(f32[4,1024,128]{2,1,0:T(8,128)} %get-tuple-element.324, s32[]{:T(128)} %get-tuple-element.322, bf16[4,512,128]{2,1,0:T(8,128)(2,1)} %get-tuple-element.338, f32[1024,512]{0,1:T(8,128)S(1)} %get-tuple-element.309, f32[1024]{0:T(1024)S(1)} %fusion.44, f32[1024]{0:T(1024)S(1)} %get-tuple-element.310), kind=kOutput, calls=%fused_computation.24.clone.1 | convolution fusion | flops 135790592 | bytes 2761728 | tf_op jit(solution)/shard_map/while/body/eval_jaxpr/dot_general | solution.py:48
  68.9 1.3 bitcast_dynamic-update-slice_fusion.5
  70.6 1.5 fusion.43
  72.4 2.2 %fusion.45 = f32[4,1024,128]{2,1,0:T(8,128)} fusion(f32[4,1024,128]{2,1,0:T(8,128)} %get-tuple-element.324, s32[]{:T(128)} %get-tuple-element.322, bf16[4,512,128]{2,1,0:T(8,128)(2,1)} %get-tuple-element.338, f32[1024,512]{0,1:T(8,128)S(1)} %get-tuple-element.309, f32[1024]{0:T(1024)S(1)} %fusion.44, f32[1024]{0:T(1024)S(1)} %get-tuple-element.310), kind=kOutput, calls=%fused_computation.24.clone.1 | convolution fusion | flops 135790592 | bytes 2761728 | tf_op jit(solution)/shard_map/while/body/eval_jaxpr/dot_general | solution.py:48
  74.7 1.3 bitcast_dynamic-update-slice_fusion.5
  76.0 1.0 copy-done.6
  77.0 1.4 copy.44
  78.5 1.2 copy.28
  80.2 4.8 %fusion.24 = f32[4,512,128]{1,2,0:T(8,128)} fusion(bf16[4,1024,512]{1,2,0:T(8,128)(2,1)} %get-tuple-element.347, bf16[4,1024,128]{1,2,0:T(8,128)(2,1)S(1)} %reshape.120), kind=kOutput, calls=%fused_computation.51 | convolution fusion | flops 536870912 | bytes 6291456 | tf_op jit(solution)/shard_map/vmap()/dot_general | solution.py:71
  85.0 1.5 broadcast.70
  86.4 31.5 %while.25 = (s32[]{:T(128)}, bf16[4,1024,512]{2,1,0:T(8,128)(2,1)}, f32[4,1024,128]{2,1,0:T(8,128)}, bf16[4,1024,512]{1,2,0:T(8,128)(2,1)}, bf16[4,1024,128]{1,2...) while((s32[]{:T(128)}, bf16[4,1024,512]{2,1,0:T(8,128)(2,1)}, ...), condition=%wide.region_6.7_spmd, body=%wide.region_4.6_spmd.sunk | while | flops 271055872 | bytes 11283049 | solution.py:113
  86.6 1.3 fusion.40
  87.9 1.3 constant_dynamic-slice_fusion.6
  89.2 0.5 copy.53
  89.8 2.4 %bitcast_dynamic-update-slice_fusion.4 = (bf16[4,1024,512]{2,1,0:T(8,128)(2,1)}, bf16[1024,512]{1,0:T(8,128)(2,1)S(1)}) fusion(bf16[4,1024,512]{2,1,0:T(8,128)(2,1)} %get-tuple-element.354, s32[]{:T(128)} %get-tuple-element.353, f32[1024]{0:T(1024)S(1)} %fusion.40, bf16[4,512,128]{2,1,0:T(8,128)(2,1)} %get-tuple-element.367, ...), kind=kOutput, calls=%fused_computation.7.clone.1 | convolution fusion | flops 136314880 | bytes 3544576 | tf_op jit(solution)/shard_map/while/body/eval_jaxpr/dot_general | solution.py:55
  92.1 2.2 %fusion.41 = f32[4,1024,128]{2,1,0:T(8,128)} fusion(f32[4,1024,128]{2,1,0:T(8,128)} %get-tuple-element.355, s32[]{:T(128)} %get-tuple-element.353, bf16[1024,512]{1,0:T(8,128)(2,1)S(1)} %get-tuple-element.298, bf16[4,512,128]{2,1,0:T(8,128)(2,1)} %get-tuple-element.369), kind=kOutput, calls=%fused_computation.6.clone.1 | convolution fusion | flops 134348800 | bytes 1704960 | tf_op jit(solution)/shard_map/while/body/eval_jaxpr/dot_general | solution.py:59
  94.5 1.3 fusion.40
  95.8 1.3 constant_dynamic-slice_fusion.6
  97.1 0.5 copy.53
  97.6 2.4 %bitcast_dynamic-update-slice_fusion.4 = (bf16[4,1024,512]{2,1,0:T(8,128)(2,1)}, bf16[1024,512]{1,0:T(8,128)(2,1)S(1)}) fusion(bf16[4,1024,512]{2,1,0:T(8,128)(2,1)} %get-tuple-element.354, s32[]{:T(128)} %get-tuple-element.353, f32[1024]{0:T(1024)S(1)} %fusion.40, bf16[4,512,128]{2,1,0:T(8,128)(2,1)} %get-tuple-element.367, ...), kind=kOutput, calls=%fused_computation.7.clone.1 | convolution fusion | flops 136314880 | bytes 3544576 | tf_op jit(solution)/shard_map/while/body/eval_jaxpr/dot_general | solution.py:55
  100.1 2.1 %fusion.41 = f32[4,1024,128]{2,1,0:T(8,128)} fusion(f32[4,1024,128]{2,1,0:T(8,128)} %get-tuple-element.355, s32[]{:T(128)} %get-tuple-element.353, bf16[1024,512]{1,0:T(8,128)(2,1)S(1)} %get-tuple-element.298, bf16[4,512,128]{2,1,0:T(8,128)(2,1)} %get-tuple-element.369), kind=kOutput, calls=%fused_computation.6.clone.1 | convolution fusion | flops 134348800 | bytes 1704960 | tf_op jit(solution)/shard_map/while/body/eval_jaxpr/dot_general | solution.py:59
  102.4 1.3 fusion.40
  103.7 1.3 constant_dynamic-slice_fusion.6
  105.0 0.5 copy.53
  105.5 2.4 %bitcast_dynamic-update-slice_fusion.4 = (bf16[4,1024,512]{2,1,0:T(8,128)(2,1)}, bf16[1024,512]{1,0:T(8,128)(2,1)S(1)}) fusion(bf16[4,1024,512]{2,1,0:T(8,128)(2,1)} %get-tuple-element.354, s32[]{:T(128)} %get-tuple-element.353, f32[1024]{0:T(1024)S(1)} %fusion.40, bf16[4,512,128]{2,1,0:T(8,128)(2,1)} %get-tuple-element.367, ...), kind=kOutput, calls=%fused_computation.7.clone.1 | convolution fusion | flops 136314880 | bytes 3544576 | tf_op jit(solution)/shard_map/while/body/eval_jaxpr/dot_general | solution.py:55
  107.9 2.1 %fusion.41 = f32[4,1024,128]{2,1,0:T(8,128)} fusion(f32[4,1024,128]{2,1,0:T(8,128)} %get-tuple-element.355, s32[]{:T(128)} %get-tuple-element.353, bf16[1024,512]{1,0:T(8,128)(2,1)S(1)} %get-tuple-element.298, bf16[4,512,128]{2,1,0:T(8,128)(2,1)} %get-tuple-element.369), kind=kOutput, calls=%fused_computation.6.clone.1 | convolution fusion | flops 134348800 | bytes 1704960 | tf_op jit(solution)/shard_map/while/body/eval_jaxpr/dot_general | solution.py:59
  110.3 1.3 fusion.40
  111.5 1.3 constant_dynamic-slice_fusion.6
  113.4 2.4 %bitcast_dynamic-update-slice_fusion.4 = (bf16[4,1024,512]{2,1,0:T(8,128)(2,1)}, bf16[1024,512]{1,0:T(8,128)(2,1)S(1)}) fusion(bf16[4,1024,512]{2,1,0:T(8,128)(2,1)} %get-tuple-element.354, s32[]{:T(128)} %get-tuple-element.353, f32[1024]{0:T(1024)S(1)} %fusion.40, bf16[4,512,128]{2,1,0:T(8,128)(2,1)} %get-tuple-element.367, ...), kind=kOutput, calls=%fused_computation.7.clone.1 | convolution fusion | flops 136314880 | bytes 3544576 | tf_op jit(solution)/shard_map/while/body/eval_jaxpr/dot_general | solution.py:55
  115.8 2.1 %fusion.41 = f32[4,1024,128]{2,1,0:T(8,128)} fusion(f32[4,1024,128]{2,1,0:T(8,128)} %get-tuple-element.355, s32[]{:T(128)} %get-tuple-element.353, bf16[1024,512]{1,0:T(8,128)(2,1)S(1)} %get-tuple-element.298, bf16[4,512,128]{2,1,0:T(8,128)(2,1)} %get-tuple-element.369), kind=kOutput, calls=%fused_computation.6.clone.1 | convolution fusion | flops 134348800 | bytes 1704960 | tf_op jit(solution)/shard_map/while/body/eval_jaxpr/dot_general | solution.py:59
  117.9 3.2 %convolution_multiply_fusion.1 = f32[4,512,128]{1,2,0:T(8,128)S(1)} fusion(bf16[4,1024,128]{1,2,0:T(8,128)(2,1)} %copy-done.3, bf16[4,1024,512]{2,1,0:T(8,128)(2,1)} %get-tuple-element.88), kind=kOutput, calls=%fused_computation.40 | convolution fusion | flops 537133056 | bytes 6291456 | tf_op jit(solution)/shard_map/vmap()/dot_general | solution.py:66
  121.5 0.9 copy-done.8
  122.7 1.5 pad_maximum_fusion
  124.3 1.6 copy-done.1
  125.9 2.5 %copy.48 = f32[4,8,128,128]{3,1,0,2:T(8,128)} copy(f32[4,8,128,128]{3,2,1,0:T(8,128)S(1)} %bitcast.143) | data formatting | bytes 4194304 | tf_op jit(solution)/shard_map/reshape | solution.py:29
  128.4 1.9 %reshape.122 = f32[1,128,4096]{2,1,0:T(8,128)S(1)} reshape(f32[128,4,8,128]{3,2,1,0:T(8,128)} %bitcast.144) | data formatting | bytes 4194304 | tf_op jit(solution)/shard_map/reshape | solution.py:31
  130.3 4.1 %copy.49 = f32[4,8,128,128]{3,1,0,2:T(8,128)} copy(f32[4,8,128,128]{3,2,1,0:T(8,128)} %bitcast.19) | data formatting | bytes 4194304 | tf_op jit(solution)/shard_map/reshape | solution.py:29
  134.4 2.9 %reshape.119 = f32[1,128,4096]{2,1,0:T(8,128)} reshape(f32[128,4,8,128]{3,2,1,0:T(8,128)} %bitcast.145) | data formatting | bytes 4194304 | tf_op jit(solution)/shard_map/reshape | solution.py:31
  137.3 1.2 add_convert_fusion
  138.5 0.8 copy-done.2
  139.5 1.2 add_convert_fusion.1
  140.7 26.7 %reduce-scatter.2.cloned.1.call-done = f32[128,1024]{1,0:T(8,128)} async-done(((f32[512,1024]{1,0:T(8,128)}), f32[128,1024]{1,0:T(8,128)}) %reduce-scatter.2.cloned.1.call-update) | async-done | bytes 524304 | tf_op jit(solution)/shard_map/reduce_scatter | solution.py:119
  167.4 1.1 convert.5
  168.5 0.7 slice_bitcast_fusion
  (53 shorter events, 6.8 us)
Async XLA Ops:
  7.2 37.7 %copy-start = (s32[1,512]{1,0:T(1,128)S(1)}, s32[1,512]{1,0:T(1,128)}, u32[]{:S(2)}) copy-start(s32[1,512]{1,0:T(1,128)} %param.14) | copy-start | bytes 6148
  7.2 37.7 %copy-start.9 = (s32[1,512]{1,0:T(1,128)S(1)}, s32[1,512]{1,0:T(1,128)}, u32[]{:S(2)}) copy-start(s32[1,512]{1,0:T(1,128)} %param.15) | copy-start | bytes 6148
  7.2 160.2 %reduce-scatter.2.cloned.1.call-start = ((), (), s32[]{:S(2)}) async-start(), calls=%async_computation.1 | async-start | bytes 2621440 | tf_op jit(solution)/shard_map/reduce_scatter | solution.py:119
  7.2 41.3 %collective-permute-start = (bf16[1,128,4096]{2,1,0:T(8,128)(2,1)}, bf16[1,128,4096]{2,1,0:T(8,128)(2,1)S(1)}, u32[]{:S(2)}, u32[]{:S(2)}) collective-permute-start(bf16[1,128,4096]{2,1,0:T(8,128)(2,1)} %param.10), channel_id=1, source_target_pairs={{24,0},{0,8},{8,16},{16,24},{25,1},{1,9},{9,17},{17,25},{26,2},{2,... | collective-permute-start | bytes 3145736 | tf_op jit(solution)/shard_map/ppermute | solution.py:12
  10.3 65.8 %collective-permute-start.1 = (bf16[1,128,4096]{2,1,0:T(8,128)(2,1)}, bf16[1,128,4096]{2,1,0:T(8,128)(2,1)S(1)}, u32[]{:S(2)}, u32[]{:S(2)}) collective-permute-start(bf16[1,128,4096]{2,1,0:T(8,128)(2,1)} %param.13), channel_id=1, source_target_pairs={{8,0},{16,8},{24,16},{0,24},{9,1},{17,9},{25,17},{1,25},{10,2},{18... | collective-permute-start | bytes 3145736 | tf_op jit(solution)/shard_map/ppermute | solution.py:12
  48.5 1.0 copy-start.4
  76.0 3.7 %copy-start.3 = (bf16[4,1024,128]{1,2,0:T(8,128)(2,1)}, bf16[4,1024,128]{1,2,0:T(8,128)(2,1)S(1)}, u32[]{:S(2)}) copy-start(bf16[4,1024,128]{1,2,0:T(8,128)(2,1)S(1)} %get-tuple-element.374) | copy-start | bytes 3145732
  76.0 1.0 copy-start.6
  121.2 1.2 copy-start.8
  124.3 1.6 copy-start.1
  134.4 2.9 %copy-start.7 = (bf16[1,128,4096]{2,1,0:T(8,128)(2,1)S(1)}, bf16[1,128,4096]{2,1,0:T(8,128)(2,1)}, u32[]{:S(2)}) copy-start(bf16[1,128,4096]{2,1,0:T(8,128)(2,1)} %copy-done.6) | copy-start | bytes 3145732
  137.3 2.0 %copy-start.2 = (f32[1,128,4096]{2,1,0:T(8,128)S(1)}, f32[1,128,4096]{2,1,0:T(8,128)}, u32[]{:S(2)}) copy-start(f32[1,128,4096]{2,1,0:T(8,128)} %reshape.119) | copy-start | bytes 6291460
  137.3 2.2 %copy-start.5 = (bf16[1,128,4096]{2,1,0:T(8,128)(2,1)S(1)}, bf16[1,128,4096]{2,1,0:T(8,128)(2,1)}, u32[]{:S(2)}) copy-start(bf16[1,128,4096]{2,1,0:T(8,128)(2,1)} %copy-done.4) | copy-start | bytes 3145732
Sparse Core Ops, SparseCore 0:
  124.4 42.9 reduce-scatter.1
where the time goes:
time: 177 us; the launch traced here: 176 us
  local copies, waits for them, and re-layouts  42.9 us (24%)
  matrix products  41 us (23%)
  blocking collectives  29.5 us (17%)
  waiting for transfers between devices  26.7 us (15%)
  other arithmetic  17.5 us (10%)
  between operations  14.2 us (8%)
  starting transfers between devices  4.08 us (2%)
    reduce_scatter x1, waiting for transfers between devices, on_device(): lax.psum_scatter(stack_terms(dkeys, dvalues), 'cp', scatter_dimension=0,...  26.7 us
    all_gather x1, blocking collectives, on_device(): lax.all_gather(keys[0], 'cp', axis=0, tiled=True)  15.2 us
    all_gather x1, blocking collectives, on_device(): lax.all_gather(values[0], 'cp', axis=0, tiled=True)  14.3 us
    unnamed x26, local copies, waits for them, and re-layouts  11 us
    dot_general x4, matrix products, backward_part(): lax.dot_general(flat_g, value, (((1,), (1,)), ((), ())), preferred_elemen...  9.64 us
    dot_general x4, matrix products, forward_part(): attended = jnp.dot(probs, value, preferred_element_type=jnp.float32)  9 us
    dot_general x4, matrix products, backward_part(): dquery = jnp.dot(dscore, key, preferred_element_type=jnp.float32) * scale  8.56 us
    dynamic_slice x8, local copies, waits for them, and re-layouts, on_device(): lax.map(lambda parts: backward_part(parts[0], parts[1], parts[2], parts[3...  7.37 us
  transfers between devices with their start and end apart: 3, of which 1 were waited for; matrix products, arithmetic and copies ran while one was open for 27% of the time, Pallas kernels for 0%

commit v1 on v0

--- a/solution.py
+++ b/solution.py
@@ -1,9 +1,34 @@
+import functools
 import jax
 import jax.numpy as jnp
 from jax import lax
 from jax.sharding import PartitionSpec as P
 
 HEAD = 128
+
+
+def unit_raise(x_part, out_dim):
+    x_part = jnp.moveaxis(x_part, 0, out_dim)
+    f_now = x_part.shape
+    y = x_part.reshape(*f_now[:out_dim], f_now[out_dim] * f_now[out_dim + 1], *f_now[out_dim + 2 :])
+    return y
+
+
+def state_corner(inp, shard_axis, k_dim):
+    n_shards = jax.lax.axis_size(shard_axis)
+    grid = [inp]
+    so_far_all = [(t, (t + 1) % n_shards) for t in range(n_shards)]
+    while len(grid) < n_shards:
+        r_now = jax.lax.ppermute(grid[-1], perm=so_far_all, axis_name=shard_axis)
+        grid.append(r_now)
+    e_next = jax.lax.axis_index(shard_axis)
+    z2 = jnp.stack(grid, 0)
+    grid = z2[(e_next - jnp.arange(n_shards)) % n_shards]
+    m_next = unit_raise(grid, k_dim)
+    return m_next
+
+
+change_rings = functools.partial(state_corner, shard_axis="cp", k_dim=0)
 
 
 def passed_along(block, axis, distance):
@@ -93,7 +118,7 @@
     cotan = passed_along(grads, "section", -1)[0]
     key_all, value_all = (
         lax.all_gather(keys[0], "cp", axis=0, tiled=True),
-        lax.all_gather(values[0], "cp", axis=0, tiled=True),
+        change_rings(values[0]),
     )
     positions = order[0]
     doc_all = jnp.take(docs[0], positions)

time: 177 us -> 171 us (0.966)
  blocking collectives: 29.5 us -> 15.7 us
  waiting for transfers between devices: 26.7 us -> 30.5 us
  starting transfers between devices: 4.08 us -> 7.75 us
    all_gather x1 -> x0, blocking collectives: 14.3 us -> none  [on_device(): lax.all_gather(values[0], 'cp', axis=0, tiled=True)]
    ppermute x0 -> x3, waiting for transfers between devices: none -> 5.64 us  [state_corner(): r_now = jax.lax.ppermute(grid[-1], perm=so_far_all, axis_name=shard_axis)]
    ppermute x0 -> x3, starting transfers between devices: none -> 4.79 us  [state_corner(): r_now = jax.lax.ppermute(grid[-1], perm=so_far_all, axis_name=shard_axis)]
    reduce_scatter x1, waiting for transfers between devices: 26.7 us -> 24.8 us  [on_device(): lax.psum_scatter(stack_terms(dkeys, dvalues), 'cp', scatter_dimension=0,...]
    unnamed x26 -> x27, local copies, waits for them, and re-layouts: 11 us -> 9.84 us
  transfers between devices with their start and end apart: 3 -> 6, of which waited for: 1 -> 2; matrix products, arithmetic and copies ran while one was open for 27% -> 28% of each run, Pallas kernels for 0% -> 0%
where the time goes in v1:
time: 171 us; the launch traced here: 170 us
  local copies, waits for them, and re-layouts  42.2 us (25%)
  matrix products  41 us (24%)
  waiting for transfers between devices  30.5 us (18%)
  other arithmetic  18.2 us (11%)
  blocking collectives  15.7 us (9%)
  between operations  14.3 us (8%)
  starting transfers between devices  7.75 us (5%)
    reduce_scatter x1, waiting for transfers between devices, on_device(): lax.psum_scatter(stack_terms(dkeys, dvalues), 'cp', scatter_dimension=0,...  24.8 us
    all_gather x1, blocking collectives, on_device(): lax.all_gather(keys[0], 'cp', axis=0, tiled=True)  15.7 us
    unnamed x27, local copies, waits for them, and re-layouts  9.84 us
    dot_general x4, matrix products, backward_part(): lax.dot_general(flat_g, value, (((1,), (1,)), ((), ())), preferred_elemen...  9.64 us
    dot_general x4, matrix products, forward_part(): attended = jnp.dot(probs, value, preferred_element_type=jnp.float32)  9 us
    dot_general x4, matrix products, backward_part(): dquery = jnp.dot(dscore, key, preferred_element_type=jnp.float32) * scale  8.54 us
    dynamic_slice x8, local copies, waits for them, and re-layouts, on_device(): lax.map(lambda parts: backward_part(parts[0], parts[1], parts[2], parts[3...  7.37 us
    reshape x2, local copies, waits for them, and re-layouts, join_heads(): rows.reshape(kv_count, group, tokens, HEAD).transpose(2, 0, 1, 3)  6.65 us
  transfers between devices with their start and end apart: 6, of which 2 were waited for; matrix products, arithmetic and copies ran while one was open for 28% of the time, Pallas kernels for 0%

profile of v1, /device:TPU:0, one launch (start us, length us, event | category | flops | bytes accessed | tf_op | source)
XLA Modules:
  0.0 170.0 jit_solution(8339416232269846386)
XLA Ops:
  7.2 3.1 %collective-permute-start.1 = (bf16[128,512]{1,0:T(8,128)(2,1)}, bf16[128,512]{1,0:T(8,128)(2,1)S(1)}, u32[]{:S(2)}, u32[]{:S(2)}) collective-permute-start(bf16[128,512]{1,0:T(8,128)(2,1)} %bitcast.162), channel_id=1, source_target_pairs={{0,2},{2,4},{4,6},{6,0},{1,3},{3,5},{5,7},{7,1},{8,10},{10,12},{12... | collective-permute-start | bytes 393224 | tf_op jit(solution)/shard_map/ppermute | solution.py:22
  10.4 1.5 collective-permute-start
  11.8 1.4 collective-permute-start.4
  13.3 0.7 compare_select_fusion.1
  14.0 1.0 copy.22
  15.0 3.5 %gather_fusion = s32[512]{0:T(512)S(1)} fusion(s32[512]{0:T(512)S(1)} %bitcast.145, s32[1024]{0:T(1024)S(1)} %pad_clamp_fusion), kind=kCustom, calls=%fused_computation | custom fusion | bytes 6144 | tf_op jit(solution)/shard_map/jit(_take)/gather | solution.py:124
  18.6 1.6 collective-permute-start.2
  20.2 15.7 %all-gather = bf16[1,512,512]{1,2,0:T(8,128)(2,1)S(1)} all-gather(bf16[1,128,512]{1,2,0:T(8,128)(2,1)S(1)} %copy.22), channel_id=2, replica_groups=mesh['section'=4,'cp'=4,'tp'=2] {'cp'}, dimensions={1}, use_global_device_ids=true | all-gather | bytes 655360 | tf_op jit(solution)/shard_map/all_gather | solution.py:120
  36.2 1.0 copy.24
  37.2 5.6 %collective-permute-done.3 = bf16[128,512]{1,0:T(8,128)(2,1)S(1)} collective-permute-done((bf16[128,512]{1,0:T(8,128)(2,1)S(1)}, bf16[128,512]{1,0:T(8,128)(2,1)S(1)}, u32[]{:S(2)}, u32[]{:S(2)}) %collective-permute-start.3) | collective-permute-done | bytes 131104 | tf_op jit(solution)/shard_map/ppermute | solution.py:22
  42.9 0.6 gather_fusion.1
  43.6 0.9 copy.25
  44.7 0.7 copy-done.4
  45.4 1.2 copy.21
  47.2 1.5 broadcast.133.clone
  48.7 23.3 %while.26 = (s32[]{:T(128)}, bf16[4,1024,512]{1,2,0:T(8,128)(2,1)}, f32[4,1024,128]{2,1,0:T(8,128)}, bf16[4,1024,128]{1,2,0:T(8,128)(2,1)S(1)}, bf16[4,512,128]{...) while((s32[]{:T(128)}, bf16[4,1024,512]{1,2,0:T(8,128)(2,1)}, ...), condition=%wide.region_3.4_spmd.clone, body=%wide.region_0.3_spmd.clone.sunk | while | flops 274397184 | bytes 11701869 | solution.py:132
  49.1 1.5 fusion.45
  50.9 2.3 %fusion.47 = f32[4,1024,128]{2,1,0:T(8,128)} fusion(f32[4,1024,128]{2,1,0:T(8,128)} %get-tuple-element.324, s32[]{:T(128)} %get-tuple-element.322, bf16[4,512,128]{2,1,0:T(8,128)(2,1)} %get-tuple-element.338, f32[1024,512]{0,1:T(8,128)S(1)} %get-tuple-element.309, f32[1024]{0:T(1024)S(1)} %fusion.46, f32[1024]{0:T(1024)S(1)} %get-tuple-element.310), kind=kOutput, calls=%fused_computation.25.clone.1 | convolution fusion | flops 135790592 | bytes 2761728 | tf_op jit(solution)/shard_map/while/body/eval_jaxpr/dot_general | solution.py:73
  53.2 1.3 bitcast_dynamic-update-slice_fusion.5
  54.9 1.5 fusion.45
  56.7 2.3 %fusion.47 = f32[4,1024,128]{2,1,0:T(8,128)} fusion(f32[4,1024,128]{2,1,0:T(8,128)} %get-tuple-element.324, s32[]{:T(128)} %get-tuple-element.322, bf16[4,512,128]{2,1,0:T(8,128)(2,1)} %get-tuple-element.338, f32[1024,512]{0,1:T(8,128)S(1)} %get-tuple-element.309, f32[1024]{0:T(1024)S(1)} %fusion.46, f32[1024]{0:T(1024)S(1)} %get-tuple-element.310), kind=kOutput, calls=%fused_computation.25.clone.1 | convolution fusion | flops 135790592 | bytes 2761728 | tf_op jit(solution)/shard_map/while/body/eval_jaxpr/dot_general | solution.py:73
  59.0 1.3 bitcast_dynamic-update-slice_fusion.5
  60.8 1.5 fusion.45
  62.6 2.2 %fusion.47 = f32[4,1024,128]{2,1,0:T(8,128)} fusion(f32[4,1024,128]{2,1,0:T(8,128)} %get-tuple-element.324, s32[]{:T(128)} %get-tuple-element.322, bf16[4,512,128]{2,1,0:T(8,128)(2,1)} %get-tuple-element.338, f32[1024,512]{0,1:T(8,128)S(1)} %get-tuple-element.309, f32[1024]{0:T(1024)S(1)} %fusion.46, f32[1024]{0:T(1024)S(1)} %get-tuple-element.310), kind=kOutput, calls=%fused_computation.25.clone.1 | convolution fusion | flops 135790592 | bytes 2761728 | tf_op jit(solution)/shard_map/while/body/eval_jaxpr/dot_general | solution.py:73
  64.8 1.3 bitcast_dynamic-update-slice_fusion.5
  66.6 1.5 fusion.45
  68.4 2.2 %fusion.47 = f32[4,1024,128]{2,1,0:T(8,128)} fusion(f32[4,1024,128]{2,1,0:T(8,128)} %get-tuple-element.324, s32[]{:T(128)} %get-tuple-element.322, bf16[4,512,128]{2,1,0:T(8,128)(2,1)} %get-tuple-element.338, f32[1024,512]{0,1:T(8,128)S(1)} %get-tuple-element.309, f32[1024]{0:T(1024)S(1)} %fusion.46, f32[1024]{0:T(1024)S(1)} %get-tuple-element.310), kind=kOutput, calls=%fused_computation.25.clone.1 | convolution fusion | flops 135790592 | bytes 2761728 | tf_op jit(solution)/shard_map/while/body/eval_jaxpr/dot_general | solution.py:73
  70.6 1.3 bitcast_dynamic-update-slice_fusion.5
  72.0 1.0 copy-done.6
  73.0 1.4 copy.43
  74.4 1.2 copy.27
  76.2 4.8 %fusion.26 = f32[4,512,128]{1,2,0:T(8,128)} fusion(bf16[4,1024,512]{1,2,0:T(8,128)(2,1)} %get-tuple-element.347, bf16[4,1024,128]{1,2,0:T(8,128)(2,1)S(1)} %reshape.165), kind=kOutput, calls=%fused_computation.60 | convolution fusion | flops 536870912 | bytes 6291456 | tf_op jit(solution)/shard_map/vmap()/dot_general | solution.py:96
  80.9 1.5 broadcast.133
  82.4 31.5 %while.25 = (s32[]{:T(128)}, bf16[4,1024,512]{2,1,0:T(8,128)(2,1)}, f32[4,1024,128]{2,1,0:T(8,128)}, bf16[4,1024,512]{1,2,0:T(8,128)(2,1)}, bf16[4,1024,128]{1,2...) while((s32[]{:T(128)}, bf16[4,1024,512]{2,1,0:T(8,128)(2,1)}, ...), condition=%wide.region_6.7_spmd, body=%wide.region_4.6_spmd.sunk | while | flops 271055872 | bytes 11283049 | solution.py:138
  82.6 1.3 fusion.42
  83.9 1.3 constant_dynamic-slice_fusion.6
  85.7 2.4 %bitcast_dynamic-update-slice_fusion.4 = (bf16[4,1024,512]{2,1,0:T(8,128)(2,1)}, bf16[1024,512]{1,0:T(8,128)(2,1)S(1)}) fusion(bf16[4,1024,512]{2,1,0:T(8,128)(2,1)} %get-tuple-element.354, s32[]{:T(128)} %get-tuple-element.353, f32[1024]{0:T(1024)S(1)} %fusion.42, bf16[4,512,128]{2,1,0:T(8,128)(2,1)} %get-tuple-element.367, ...), kind=kOutput, calls=%fused_computation.8.clone.1 | convolution fusion | flops 136314880 | bytes 3544576 | tf_op jit(solution)/shard_map/while/body/eval_jaxpr/dot_general | solution.py:80
  88.1 2.1 %fusion.43 = f32[4,1024,128]{2,1,0:T(8,128)} fusion(f32[4,1024,128]{2,1,0:T(8,128)} %get-tuple-element.355, s32[]{:T(128)} %get-tuple-element.353, bf16[1024,512]{1,0:T(8,128)(2,1)S(1)} %get-tuple-element.298, bf16[4,512,128]{2,1,0:T(8,128)(2,1)} %get-tuple-element.369), kind=kOutput, calls=%fused_computation.7.clone.1 | convolution fusion | flops 134348800 | bytes 1704960 | tf_op jit(solution)/shard_map/while/body/eval_jaxpr/dot_general | solution.py:84
  90.5 1.3 fusion.42
  91.7 1.3 constant_dynamic-slice_fusion.6
  93.6 2.4 %bitcast_dynamic-update-slice_fusion.4 = (bf16[4,1024,512]{2,1,0:T(8,128)(2,1)}, bf16[1024,512]{1,0:T(8,128)(2,1)S(1)}) fusion(bf16[4,1024,512]{2,1,0:T(8,128)(2,1)} %get-tuple-element.354, s32[]{:T(128)} %get-tuple-element.353, f32[1024]{0:T(1024)S(1)} %fusion.42, bf16[4,512,128]{2,1,0:T(8,128)(2,1)} %get-tuple-element.367, ...), kind=kOutput, calls=%fused_computation.8.clone.1 | convolution fusion | flops 136314880 | bytes 3544576 | tf_op jit(solution)/shard_map/while/body/eval_jaxpr/dot_general | solution.py:80
  96.0 2.1 %fusion.43 = f32[4,1024,128]{2,1,0:T(8,128)} fusion(f32[4,1024,128]{2,1,0:T(8,128)} %get-tuple-element.355, s32[]{:T(128)} %get-tuple-element.353, bf16[1024,512]{1,0:T(8,128)(2,1)S(1)} %get-tuple-element.298, bf16[4,512,128]{2,1,0:T(8,128)(2,1)} %get-tuple-element.369), kind=kOutput, calls=%fused_computation.7.clone.1 | convolution fusion | flops 134348800 | bytes 1704960 | tf_op jit(solution)/shard_map/while/body/eval_jaxpr/dot_general | solution.py:84
  98.3 1.3 fusion.42
  99.6 1.3 constant_dynamic-slice_fusion.6
  101.5 2.4 %bitcast_dynamic-update-slice_fusion.4 = (bf16[4,1024,512]{2,1,0:T(8,128)(2,1)}, bf16[1024,512]{1,0:T(8,128)(2,1)S(1)}) fusion(bf16[4,1024,512]{2,1,0:T(8,128)(2,1)} %get-tuple-element.354, s32[]{:T(128)} %get-tuple-element.353, f32[1024]{0:T(1024)S(1)} %fusion.42, bf16[4,512,128]{2,1,0:T(8,128)(2,1)} %get-tuple-element.367, ...), kind=kOutput, calls=%fused_computation.8.clone.1 | convolution fusion | flops 136314880 | bytes 3544576 | tf_op jit(solution)/shard_map/while/body/eval_jaxpr/dot_general | solution.py:80
  103.9 2.1 %fusion.43 = f32[4,1024,128]{2,1,0:T(8,128)} fusion(f32[4,1024,128]{2,1,0:T(8,128)} %get-tuple-element.355, s32[]{:T(128)} %get-tuple-element.353, bf16[1024,512]{1,0:T(8,128)(2,1)S(1)} %get-tuple-element.298, bf16[4,512,128]{2,1,0:T(8,128)(2,1)} %get-tuple-element.369), kind=kOutput, calls=%fused_computation.7.clone.1 | convolution fusion | flops 134348800 | bytes 1704960 | tf_op jit(solution)/shard_map/while/body/eval_jaxpr/dot_general | solution.py:84
  106.2 1.3 fusion.42
  107.5 1.3 constant_dynamic-slice_fusion.6
  109.3 2.4 %bitcast_dynamic-update-slice_fusion.4 = (bf16[4,1024,512]{2,1,0:T(8,128)(2,1)}, bf16[1024,512]{1,0:T(8,128)(2,1)S(1)}) fusion(bf16[4,1024,512]{2,1,0:T(8,128)(2,1)} %get-tuple-element.354, s32[]{:T(128)} %get-tuple-element.353, f32[1024]{0:T(1024)S(1)} %fusion.42, bf16[4,512,128]{2,1,0:T(8,128)(2,1)} %get-tuple-element.367, ...), kind=kOutput, calls=%fused_computation.8.clone.1 | convolution fusion | flops 136314880 | bytes 3544576 | tf_op jit(solution)/shard_map/while/body/eval_jaxpr/dot_general | solution.py:80
  111.7 2.1 %fusion.43 = f32[4,1024,128]{2,1,0:T(8,128)} fusion(f32[4,1024,128]{2,1,0:T(8,128)} %get-tuple-element.355, s32[]{:T(128)} %get-tuple-element.353, bf16[1024,512]{1,0:T(8,128)(2,1)S(1)} %get-tuple-element.298, bf16[4,512,128]{2,1,0:T(8,128)(2,1)} %get-tuple-element.369), kind=kOutput, calls=%fused_computation.7.clone.1 | convolution fusion | flops 134348800 | bytes 1704960 | tf_op jit(solution)/shard_map/while/body/eval_jaxpr/dot_general | solution.py:84
  113.9 3.2 %convolution_multiply_fusion.1 = f32[4,512,128]{1,2,0:T(8,128)S(1)} fusion(bf16[4,1024,128]{1,2,0:T(8,128)(2,1)} %copy-done.3, bf16[4,1024,512]{2,1,0:T(8,128)(2,1)} %get-tuple-element.88), kind=kOutput, calls=%fused_computation.41 | convolution fusion | flops 537133056 | bytes 6291456 | tf_op jit(solution)/shard_map/vmap()/dot_general | solution.py:91
  117.5 0.9 copy-done.8
  118.7 1.5 pad_maximum_fusion
  120.2 1.6 copy-done.1
  121.8 2.5 %copy.47 = f32[4,8,128,128]{3,1,0,2:T(8,128)} copy(f32[4,8,128,128]{3,2,1,0:T(8,128)S(1)} %bitcast.147) | data formatting | bytes 4194304 | tf_op jit(solution)/shard_map/reshape | solution.py:54
  124.3 1.7 %reshape.167 = f32[1,128,4096]{2,1,0:T(8,128)S(1)} reshape(f32[128,4,8,128]{3,2,1,0:T(8,128)} %bitcast.148) | data formatting | bytes 4194304 | tf_op jit(solution)/shard_map/reshape | solution.py:56
  126.1 4.1 %copy.48 = f32[4,8,128,128]{3,1,0,2:T(8,128)} copy(f32[4,8,128,128]{3,2,1,0:T(8,128)} %bitcast.23) | data formatting | bytes 4194304 | tf_op jit(solution)/shard_map/reshape | solution.py:54
  130.2 2.8 %reshape.164 = f32[1,128,4096]{2,1,0:T(8,128)} reshape(f32[128,4,8,128]{3,2,1,0:T(8,128)} %bitcast.149) | data formatting | bytes 4194304 | tf_op jit(solution)/shard_map/reshape | solution.py:56
  133.1 1.2 add_convert_fusion
  134.3 0.8 copy-done.2
  135.3 1.2 add_convert_fusion.1
  136.5 24.8 %reduce-scatter.2.cloned.1.call-done = f32[128,1024]{1,0:T(8,128)} async-done(((f32[512,1024]{1,0:T(8,128)}), f32[128,1024]{1,0:T(8,128)}) %reduce-scatter.2.cloned.1.call-update) | async-done | bytes 524304 | tf_op jit(solution)/shard_map/reduce_scatter | solution.py:144
  161.3 1.1 convert.5
  162.4 0.7 slice_bitcast_fusion
  (64 shorter events, 8.7 us)
Async XLA Ops:
  7.2 7.8 %copy-start = (s32[1,512]{1,0:T(1,128)S(1)}, s32[1,512]{1,0:T(1,128)}, u32[]{:S(2)}) copy-start(s32[1,512]{1,0:T(1,128)} %param.14) | copy-start | bytes 6148
  7.2 35.6 %copy-start.10 = (bf16[1,128,512]{2,1,0:T(8,128)(2,1)S(1)}, bf16[1,128,512]{2,1,0:T(8,128)(2,1)}, u32[]{:S(2)}) copy-start(bf16[1,128,512]{2,1,0:T(8,128)(2,1)} %param.12) | copy-start | bytes 393220
  7.2 11.3 %copy-start.9 = (s32[1,512]{1,0:T(1,128)S(1)}, s32[1,512]{1,0:T(1,128)}, u32[]{:S(2)}) copy-start(s32[1,512]{1,0:T(1,128)} %param.15) | copy-start | bytes 6148
  7.2 154.1 %reduce-scatter.2.cloned.1.call-start = ((), (), s32[]{:S(2)}) async-start(), calls=%async_computation.1 | async-start | bytes 2621440 | tf_op jit(solution)/shard_map/reduce_scatter | solution.py:144
  7.2 11.3 %collective-permute-start.1 = (bf16[128,512]{1,0:T(8,128)(2,1)}, bf16[128,512]{1,0:T(8,128)(2,1)S(1)}, u32[]{:S(2)}, u32[]{:S(2)}) collective-permute-start(bf16[128,512]{1,0:T(8,128)(2,1)} %bitcast.162), channel_id=1, source_target_pairs={{0,2},{2,4},{4,6},{6,0},{1,3},{3,5},{5,7},{7,1},{8,10},{10,12},{12... | collective-permute-start | bytes 393224 | tf_op jit(solution)/shard_map/ppermute | solution.py:22
  10.4 34.1 %collective-permute-start = (bf16[1,128,4096]{2,1,0:T(8,128)(2,1)}, bf16[1,128,4096]{2,1,0:T(8,128)(2,1)S(1)}, u32[]{:S(2)}, u32[]{:S(2)}) collective-permute-start(bf16[1,128,4096]{2,1,0:T(8,128)(2,1)} %param.10), channel_id=1, source_target_pairs={{24,0},{0,8},{8,16},{16,24},{25,1},{1,9},{9,17},{17,25},{26,2},{2,... | collective-permute-start | bytes 3145736 | tf_op jit(solution)/shard_map/ppermute | solution.py:37
  11.8 60.1 %collective-permute-start.4 = (bf16[1,128,4096]{2,1,0:T(8,128)(2,1)}, bf16[1,128,4096]{2,1,0:T(8,128)(2,1)S(1)}, u32[]{:S(2)}, u32[]{:S(2)}) collective-permute-start(bf16[1,128,4096]{2,1,0:T(8,128)(2,1)} %param.13), channel_id=1, source_target_pairs={{8,0},{16,8},{24,16},{0,24},{9,1},{17,9},{25,17},{1,25},{10,2},{18... | collective-permute-start | bytes 3145736 | tf_op jit(solution)/shard_map/ppermute | solution.py:37
  18.6 17.4 %collective-permute-start.2 = (bf16[128,512]{1,0:T(8,128)(2,1)S(1)}, bf16[128,512]{1,0:T(8,128)(2,1)S(1)}, u32[]{:S(2)}, u32[]{:S(2)}) collective-permute-start(bf16[128,512]{1,0:T(8,128)(2,1)S(1)} %collective-permute-done.1), channel_id=1, source_target_pairs={{0,2},{2,4},{4,6},{6,0},{1,3},{3,5},{5,7},{7,1},{8,10},{10,12},{12... | collective-permute-start | bytes 393224 | tf_op jit(solution)/shard_map/ppermute | solution.py:22
  36.0 6.8 %collective-permute-start.3 = (bf16[128,512]{1,0:T(8,128)(2,1)S(1)}, bf16[128,512]{1,0:T(8,128)(2,1)S(1)}, u32[]{:S(2)}, u32[]{:S(2)}) collective-permute-start(bf16[128,512]{1,0:T(8,128)(2,1)S(1)} %collective-permute-done.2), channel_id=1, source_target_pairs={{0,2},{2,4},{4,6},{6,0},{1,3},{3,5},{5,7},{7,1},{8,10},{10,12},{12... | collective-permute-start | bytes 393224 | tf_op jit(solution)/shard_map/ppermute | solution.py:22
  44.5 1.0 copy-start.4
  72.0 3.7 %copy-start.3 = (bf16[4,1024,128]{1,2,0:T(8,128)(2,1)}, bf16[4,1024,128]{1,2,0:T(8,128)(2,1)S(1)}, u32[]{:S(2)}) copy-start(bf16[4,1024,128]{1,2,0:T(8,128)(2,1)S(1)} %get-tuple-element.374) | copy-start | bytes 3145732
  72.0 1.0 copy-start.6
  117.1 1.2 copy-start.8
  120.2 1.6 copy-start.1
  130.2 2.9 %copy-start.7 = (bf16[1,128,4096]{2,1,0:T(8,128)(2,1)S(1)}, bf16[1,128,4096]{2,1,0:T(8,128)(2,1)}, u32[]{:S(2)}) copy-start(bf16[1,128,4096]{2,1,0:T(8,128)(2,1)} %copy-done.6) | copy-start | bytes 3145732
  133.1 2.0 %copy-start.2 = (f32[1,128,4096]{2,1,0:T(8,128)S(1)}, f32[1,128,4096]{2,1,0:T(8,128)}, u32[]{:S(2)}) copy-start(f32[1,128,4096]{2,1,0:T(8,128)} %reshape.164) | copy-start | bytes 6291460
  133.1 2.2 %copy-start.5 = (bf16[1,128,4096]{2,1,0:T(8,128)(2,1)S(1)}, bf16[1,128,4096]{2,1,0:T(8,128)(2,1)}, u32[]{:S(2)}) copy-start(bf16[1,128,4096]{2,1,0:T(8,128)(2,1)} %copy-done.4) | copy-start | bytes 3145732
Sparse Core Ops, SparseCore 0:
  120.4 40.9 reduce-scatter.1
